TPU v7x, 32 devices: a whole 2x2x4 slice. The times are simulated.
32 devices in a mesh: orb: 8 (over y, x, core), walk: 4 (over z).
Axes of the slice: x: 2, y: 2, z: 4, core: 2. Of those that a mesh axis runs over, the one named last changes fastest.
Arguments:
- chol: bfloat16 [32, 2048, 2048], P(None, 'orb', 'walk'), may hold values from -6 to 6
- orbitals: bfloat16 [2048, 1024], replicated, may hold values from -0.125 to 0.125
- greens: bfloat16 [4, 1024, 2048], P('walk'), may hold values from -0.00390625 to 0.00390625
- shift: float32 [32], P('orb'), may hold values from -6 to 6
Outputs:
- force_bias: float32 [4, 32], P('walk', 'orb')
- rotated: bfloat16 [32, 1024, 2048], P('orb', None, 'walk')
All inputs are finite; a program needn't handle non-finite values.
Results may differ from a plain program's by a relative error of at most 0.007.
Values may be sent and summed in bfloat16 or wider, within the bound.
A program may use at most 64 MiB of HBM per device.

v0:
```python
import functools

import jax
import jax.numpy as jnp
from jax import lax
from jax.experimental import pallas as pl
from jax.experimental.pallas import tpu as pltpu
from jax.sharding import PartitionSpec as P

MESH = pl.DeviceIdType.MESH
LANES = 128


def xor(a, b, size):
    total, bit = 0, 1
    while bit < size:
        total = total + ((a // bit + b // bit) % 2) * bit
        bit *= 2
    return total


def kernel(
    n, m, chol, orbitals, greens, bias_out, rotated,
    chunks, chol_v, orb_v, orb_t, greens_v, products, arrived, acc,
    terms, terms_in, sums, sums_in,
    local_sem, send_sem, recv_sem, walk_send, walk_recv,
    term_send, term_recv, sum_send, sum_recv,
):
    me, my_walk = lax.axis_index("orb"), lax.axis_index("walk")
    vectors, rows, cols = chol.shape
    owned = vectors // n
    walkers = greens.shape[0]
    core = me % 2

    loads = [
        pltpu.make_async_copy(greens, greens_v, local_sem.at[0]),
        pltpu.make_async_copy(orbitals, orb_v, local_sem.at[1]),
        pltpu.make_async_copy(chol, chol_v, local_sem.at[2]),
    ]

    barrier = pltpu.get_barrier_semaphore()
    for k in range(1, n):
        pl.semaphore_signal(barrier, inc=1, device_id={"orb": xor(me, k, n)}, device_id_type=MESH)
    for k in range(1, m):
        pl.semaphore_signal(
            barrier, inc=1, device_id={"walk": (my_walk + k) % m}, device_id_type=MESH
        )
    pl.semaphore_wait(barrier, n + m - 2)

    def chunk_copy(g, k):
        peer = xor(me, k, n)
        return pltpu.make_async_remote_copy(
            src_ref=chol.at[peer * owned + g],
            dst_ref=chunks.at[k, g],
            send_sem=send_sem.at[k, g],
            recv_sem=recv_sem.at[k, g],
            device_id={"orb": peer},
            device_id_type=MESH,
        )

    def send_vector(g):
        half = n // 2
        for low in range(2):
            if low == 1:
                chunk_copy(g, 1).start()
            for high in range(1, half):
                chip = high + core * (half - 2 * high)
                chunk_copy(g, chip * 2 + low).start()

    early = max(owned - 1, 1)
    for g in range(early):
        send_vector(g)

    for load in loads:
        load.start()
    loads[0].wait()
    loads[1].wait()
    my_rows = orb_v[pl.ds(pl.multiple_of(me * rows, rows), rows), :]
    for w in range(walkers):
        for j in range(m):
            products[j, w] = jnp.dot(
                my_rows, greens_v[w, :, j * cols : (j + 1) * cols],
                preferred_element_type=jnp.float32,
            ).astype(products.dtype)

    def turn(s, _):
        orb_t[s] = orb_v[pl.ds(pl.multiple_of(s * rows, rows), rows), :].T
        return _

    lax.fori_loop(0, n, turn, 0)

    def walk_copy(k):
        peer = (my_walk + k) % m
        return pltpu.make_async_remote_copy(
            src_ref=products.at[peer],
            dst_ref=arrived.at[m - k],
            send_sem=walk_send.at[k],
            recv_sem=walk_recv.at[m - k],
            device_id={"walk": peer},
            device_id_type=MESH,
        )

    def walk_arrival(k):
        return pltpu.make_async_remote_copy(
            src_ref=products.at[0],
            dst_ref=arrived.at[k],
            send_sem=walk_send.at[k],
            recv_sem=walk_recv.at[k],
            device_id={"walk": (my_walk + k) % m},
            device_id_type=MESH,
        )

    for k in range(1, m):
        walk_copy(k).start()

    loads[2].wait()

    def begin(g, _):
        acc[g] = jnp.dot(orb_t[me], chol_v[me * owned + g], preferred_element_type=jnp.float32)
        return _

    lax.fori_loop(0, owned, begin, 0)
    arrived[0] = products[my_walk]
    for k in range(1, m):
        walk_arrival(k).wait_recv()

    def term(v, _):
        block = chol_v[v].astype(jnp.float32)
        for k in range(m):
            from_walk = (my_walk + k) % m
            for w in range(walkers):
                both = block * arrived[k, w].astype(jnp.float32)
                both = jnp.sum(both, axis=0, keepdims=True)
                part = both[:, :LANES]
                for start in range(LANES, cols, LANES):
                    part = part + both[:, start : start + LANES]
                terms[v // owned, from_walk, w, pl.ds(v % owned, 1), :] = part
        return _

    lax.fori_loop(0, vectors, term, 0)

    def take(g, k):
        chunk_copy(g, k).wait_recv()
        return acc[g] + jnp.dot(
            orb_t[xor(me, k, n)], chunks[k, g], preferred_element_type=jnp.float32
        )

    def add(g):
        def step(k, _):
            acc[g] = take(g, k)
            return _

        return step

    def finish(g):
        rotated[g] = take(g, n - 1).astype(rotated.dtype)

    def term_copy(k):
        peer = xor(me, k, n)
        return pltpu.make_async_remote_copy(
            src_ref=terms.at[peer],
            dst_ref=terms_in.at[k],
            send_sem=term_send.at[k],
            recv_sem=term_recv.at[k],
            device_id={"orb": peer},
            device_id_type=MESH,
        )

    def sum_copy(k):
        peer = (my_walk + k) % m
        return pltpu.make_async_remote_copy(
            src_ref=sums.at[peer],
            dst_ref=sums_in.at[m - k],
            send_sem=sum_send.at[k],
            recv_sem=sum_recv.at[m - k],
            device_id={"walk": peer},
            device_id_type=MESH,
        )

    def sum_arrival(k):
        return pltpu.make_async_remote_copy(
            src_ref=sums.at[0],
            dst_ref=sums_in.at[k],
            send_sem=sum_send.at[k],
            recv_sem=sum_recv.at[k],
            device_id={"walk": (my_walk + k) % m},
            device_id_type=MESH,
        )

    lax.fori_loop(1, n - 1, add(0), 0)
    for k in range(1, n):
        term_copy(k).start()
    for g in range(early, owned):
        send_vector(g)
    if owned > 1:
        finish(0)

    if owned > 2:
        def vector(g, _):
            lax.fori_loop(1, n - 1, add(g), 0)
            finish(g)
            return _

        lax.fori_loop(1, owned - 1, vector, 0)

    def drain(g, _):
        def one(k, _):
            chunk_copy(g, k).wait_send()
            return _

        return lax.fori_loop(1, n, one, _)

    last = owned - 1
    lax.fori_loop(0, last, drain, 0)
    for k in range(1, m):
        walk_copy(k).wait_send()
    for k in range(1, n):
        term_copy(k).wait_send()

    mine = terms[me]
    for k in range(1, n):
        term_copy(k).wait_recv()
        mine = mine + terms_in[k]
    sums[...] = mine
    if owned > 1:
        lax.fori_loop(1, 2, add(last), 0)
    for k in range(1, m):
        sum_copy(k).start()
    if owned > 1:
        lax.fori_loop(2, n - 1, add(last), 0)
    total = sums[my_walk]
    for k in range(1, m):
        sum_arrival(k).wait_recv()
        total = total + sums_in[k]
    bias_out[...] = jnp.sum(total, axis=-1)
    finish(last)

    for k in range(1, m):
        sum_copy(k).wait_send()
    drain(last, 0)


def store(bias, shift, rounded, bias_out, rotated, sems):
    writes = [
        pltpu.make_async_copy(rounded.at[g], rotated.at[g], sems.at[g])
        for g in range(rounded.shape[0])
    ]
    for write in writes:
        write.start()
    bias_out[...] = bias[...] - shift[...]
    for write in writes:
        write.wait()


def local(n, m, chol, orbitals, greens, shift):
    vectors, rows, cols = chol.shape
    owned = vectors // n
    walkers, occupied, _ = greens.shape
    bf16, f32 = jnp.bfloat16, jnp.float32
    dma = pltpu.SemaphoreType.DMA
    any_space = pl.BlockSpec(memory_space=pl.ANY)
    vmem = pl.BlockSpec(memory_space=pltpu.VMEM)
    bias, rounded = pl.pallas_call(
        functools.partial(kernel, n, m),
        out_shape=(
            pltpu.VMEM((walkers, owned), f32),
            pltpu.VMEM((owned, occupied, cols), bf16),
        ),
        in_specs=[any_space] * 3,
        out_specs=(vmem, vmem),
        scratch_shapes=[
            pltpu.VMEM((n, owned, rows, cols), bf16),
            pltpu.VMEM(chol.shape, bf16),
            pltpu.VMEM(orbitals.shape, bf16),
            pltpu.VMEM((n, occupied, rows), bf16),
            pltpu.VMEM(greens.shape, bf16),
            pltpu.VMEM((m, walkers, rows, cols), bf16),
            pltpu.VMEM((m, walkers, rows, cols), bf16),
            pltpu.VMEM((owned, occupied, cols), f32),
            pltpu.VMEM((n, m, walkers, owned, LANES), f32),
            pltpu.VMEM((n, m, walkers, owned, LANES), f32),
            pltpu.VMEM((m, walkers, owned, LANES), f32),
            pltpu.VMEM((m, walkers, owned, LANES), f32),
            dma((3,)),
            dma((n, owned)),
            dma((n, owned)),
            dma((m,)),
            dma((m,)),
            dma((n,)),
            dma((n,)),
            dma((m,)),
            dma((m,)),
        ],
        compiler_params=pltpu.CompilerParams(
            collective_id=0, has_side_effects=True, vmem_limit_bytes=59 * 2**20
        ),
    )(chol, orbitals, greens)
    return pl.pallas_call(
        store,
        out_shape=(
            jax.ShapeDtypeStruct((walkers, owned), f32),
            jax.ShapeDtypeStruct((owned, occupied, cols), bf16),
        ),
        in_specs=[vmem, vmem, vmem],
        out_specs=(vmem, any_space),
        scratch_shapes=[dma((owned,))],
        compiler_params=pltpu.CompilerParams(vmem_limit_bytes=2**20),
    )(bias, shift.reshape(1, owned), rounded)


def solution(mesh):
    in_specs = (P(None, "orb", "walk"), P(), P("walk", None, None), P("orb"))
    out_specs = (P("walk", "orb"), P("orb", None, "walk"))
    body = functools.partial(local, mesh.shape["orb"], mesh.shape["walk"])
    return jax.shard_map(body, mesh=mesh, in_specs=in_specs, out_specs=out_specs, check_vma=False)
```

profile of v0, /device:TPU:1, one launch (start us, length us, event | category | flops | bytes accessed | tf_op | source)
XLA Modules:
  0.0 103.1 jit_solution(16719984597222007710)
XLA Ops:
  0.6 0.0 copy-start
  0.6 99.9 %shard_map.59 = (f32[1,4]{1,0:T(1,128)S(1)}, bf16[4,1024,512]{2,1,0:T(8,128)(2,1)S(1)}) custom-call(bf16[32,256,512]{2,1,0:T(8,128)(2,1)} %chol.1, bf16[2048,1024]{1,0:T(8,128)(2,1)} %orbitals.1, bf16[1,1024,2048]{2,1,0:T(8,128)(2,1)} %greens.1), custom_call_target="tpu_custom_call" | custom-call | tf_op jit(solution)/shard_map/pallas_call | solution.py:263
  100.6 0.0 copy-done
  100.6 2.6 %shard_map.60 = (f32[1,4]{1,0:T(1,128)}, bf16[4,1024,512]{2,1,0:T(8,128)(2,1)}) custom-call(f32[1,4]{1,0:T(1,128)S(1)} %get-tuple-element.4.bias, f32[1,4]{1,0:T(1,128)S(1)} %bitcast.1, bf16[4,1024,512]{2,1,0:T(8,128)(2,1)S(1)} %get-tuple-element.5.rounded), custom_call_target="tpu_custom_call" | custom-call | tf_op jit(solution)/shard_map/pallas_call | solution.py:298
Async XLA Ops:
  0.6 99.9 %copy-start = (f32[4]{0:T(128)S(1)}, f32[4]{0:T(128)}, u32[]{:S(2)}) copy-start(f32[4]{0:T(128)} %param.7) | copy-start | bytes 52
where the time goes:
time: 104 us; the launch traced here: 103 us
  Pallas kernels  102 us (98%)
    pallas_call x1, Pallas kernels, local(): pl.pallas_call(functools.partial(kernel, n, m), out_shape=(pltpu.VMEM((wa...  99.9 us
    pallas_call x1, Pallas kernels, local(): pl.pallas_call(store, out_shape=(jax.ShapeDtypeStruct((walkers, owned), f...  2.55 us

commit v1 on v0

v1 whole, which is shorter than its diff:
```python
import functools

import jax
import jax.numpy as jnp
from jax import lax
from jax.experimental import pallas as pl
from jax.experimental.pallas import tpu as pltpu
from jax.sharding import PartitionSpec as P

MESH = pl.DeviceIdType.MESH
LANES = 128


def xor(a, b, size):
    total, bit = 0, 1
    while bit < size:
        total = total + ((a // bit + b // bit) % 2) * bit
        bit *= 2
    return total


def low_bit(k):
    return k & -k


def ones(k):
    return bin(k).count("1")


def kernel(
    n, m, chol, orbitals, greens, shift, bias_out, rotated,
    chunks, first_v, chol_v, orb_v, orb_t, greens_v, products, arrived, acc,
    rows_v, terms, terms_in, sums, sums_in,
    local_sem, send_sem, recv_sem, walk_send, walk_recv,
    term_send, term_recv, sum_send, sum_recv, heard, chain,
):
    me, my_walk = lax.axis_index("orb"), lax.axis_index("walk")
    vectors, rows, cols = chol.shape
    owned = vectors // n
    walkers = greens.shape[0]
    half = n // 2
    leader = me == n - 1
    has_below, has_above = my_walk > 0, my_walk < m - 1
    bits = [1 << b for b in range(n.bit_length() - 1)]
    share = m * walkers * owned

    barrier = pltpu.get_barrier_semaphore()
    for bit in reversed(bits):
        pl.semaphore_signal(barrier, inc=1, device_id={"orb": xor(me, bit, n)}, device_id_type=MESH)

    def greet(other):
        pl.semaphore_signal(barrier, inc=1, device_id={"walk": other}, device_id_type=MESH)

    pl.when(leader & has_below)(lambda: greet(my_walk - 1))
    pl.when(leader & has_above)(lambda: greet(my_walk + 1))

    firsts = [
        pltpu.make_async_copy(chol.at[xor(me, bit, n) * owned], first_v.at[i], local_sem.at[3 + i])
        for i, bit in enumerate(bits[1:])
    ]
    for load in firsts:
        load.start()
    loads = [
        pltpu.make_async_copy(greens, greens_v, local_sem.at[0]),
        pltpu.make_async_copy(orbitals, orb_v, local_sem.at[1]),
        pltpu.make_async_copy(chol, chol_v, local_sem.at[2]),
    ]

    planes = (my_walk + m - 1) // m + (2 * m - 2 - my_walk) // m
    pl.semaphore_wait(barrier, len(bits) + me // (n - 1) * planes)

    def tell(k):
        peer = xor(me, low_bit(k), n)
        pl.semaphore_signal(heard.at[k], inc=1, device_id={"orb": peer}, device_id_type=MESH)

    def hear(k):
        if ones(k) > 1:
            pl.semaphore_wait(heard.at[k], 1)
        for further in range(k + 1, n):
            if ones(further) == ones(k) + 1 and further - low_bit(further) == k:
                tell(further)

    for bit in bits:
        hear(bit)

    def chunk_copy(g, k, src=None):
        peer = xor(me, k, n)
        return pltpu.make_async_remote_copy(
            src_ref=chol.at[peer * owned + g] if src is None else src,
            dst_ref=chunks.at[k, g],
            send_sem=send_sem.at[k, g],
            recv_sem=recv_sem.at[k, g],
            device_id={"orb": peer},
            device_id_type=MESH,
        )

    def send_vector(g):
        for low in range(2):
            if low == 1:
                chunk_copy(g, 1).start()
            for chip in range(half - 1, 0, -1):
                chunk_copy(g, chip * 2 + low).start()

    for i, bit in enumerate(bits[1:]):
        firsts[i].wait()
        chunk_copy(0, bit, first_v.at[i]).start()
    chunk_copy(0, 1).start()
    for low in range(2):
        for k in range(2 + low, n, 2):
            if ones(k) > 1:
                hear(k)
                chunk_copy(0, k).start()
    early = max(owned - 1, 1)
    for g in range(1, early):
        send_vector(g)

    for load in loads:
        load.start()

    def pass_on(i, other):
        pl.semaphore_signal(chain.at[i], inc=1, device_id={"walk": other}, device_id_type=MESH)

    pl.when(leader & has_below)(lambda: pl.semaphore_wait(chain.at[0], 1))
    pl.when(leader & has_above)(lambda: pass_on(0, my_walk + 1))
    pl.when(leader & has_above)(lambda: pl.semaphore_wait(chain.at[1], 1))
    pl.when(leader & has_below)(lambda: pass_on(1, my_walk - 1))

    @pl.when(leader)
    def _():
        for k in range(1, n):
            pl.semaphore_signal(
                chain.at[2], inc=1, device_id={"orb": xor(me, k, n)}, device_id_type=MESH
            )

    loads[0].wait()
    loads[1].wait()
    my_rows = orb_v[pl.ds(pl.multiple_of(me * rows, rows), rows), :]
    for w in range(walkers):
        for j in range(m):
            products[j, w] = jnp.dot(
                my_rows, greens_v[w, :, j * cols : (j + 1) * cols],
                preferred_element_type=jnp.float32,
            ).astype(products.dtype)

    def turn(s, _):
        orb_t[s] = orb_v[pl.ds(pl.multiple_of(s * rows, rows), rows), :].T
        return _

    lax.fori_loop(0, n, turn, 0)

    def walk_copy(k):
        peer = (my_walk + k) % m
        return pltpu.make_async_remote_copy(
            src_ref=products.at[peer],
            dst_ref=arrived.at[m - k],
            send_sem=walk_send.at[k],
            recv_sem=walk_recv.at[m - k],
            device_id={"walk": peer},
            device_id_type=MESH,
        )

    def walk_arrival(k):
        return pltpu.make_async_remote_copy(
            src_ref=products.at[0],
            dst_ref=arrived.at[k],
            send_sem=walk_send.at[k],
            recv_sem=walk_recv.at[k],
            device_id={"walk": (my_walk + k) % m},
            device_id_type=MESH,
        )

    pl.when(me < n - 1)(lambda: pl.semaphore_wait(chain.at[2], 1))
    for k in range(1, m):
        walk_copy(k).start()

    loads[2].wait()

    def begin(g, _):
        acc[g] = jnp.dot(orb_t[me], chol_v[me * owned + g], preferred_element_type=jnp.float32)
        return _

    lax.fori_loop(0, owned, begin, 0)
    arrived[0] = products[my_walk]
    for k in range(1, m):
        walk_arrival(k).wait_recv()

    def term(v, _):
        block = chol_v[v].astype(jnp.float32)
        start = (v // owned) * share + v % owned
        for k in range(m):
            from_walk = (my_walk + k) % m
            for w in range(walkers):
                both = block * arrived[k, w].astype(jnp.float32)
                both = jnp.sum(both, axis=0, keepdims=True)
                part = both[:, :LANES]
                for lane in range(LANES, cols, LANES):
                    part = part + both[:, lane : lane + LANES]
                rows_v[pl.ds(start + (from_walk * walkers + w) * owned, 1), :] = part
        return _

    lax.fori_loop(0, vectors, term, 0)
    for b in range(terms.shape[0]):
        turned = rows_v[b * LANES : (b + 1) * LANES, :].T
        terms[b] = jnp.sum(turned, axis=0, keepdims=True)

    def take(g, k):
        chunk_copy(g, k).wait_recv()
        return acc[g] + jnp.dot(
            orb_t[xor(me, k, n)], chunks[k, g], preferred_element_type=jnp.float32
        )

    def arrival(i):
        return (half - 1 - i % (half - 1)) * 2 + i // (half - 1)

    steps = 2 * (half - 1)

    def add(g, k):
        acc[g] = take(g, k)

    def add_some(g, start, stop):
        def step(i, _):
            add(g, arrival(i))
            return _

        lax.fori_loop(start, stop, step, 0)

    def finish(g):
        rotated[g] = take(g, arrival(steps - 1)).astype(rotated.dtype)

    def term_copy(k):
        peer = xor(me, k, n)
        return pltpu.make_async_remote_copy(
            src_ref=terms.at[peer * share // LANES],
            dst_ref=terms_in.at[k],
            send_sem=term_send.at[k],
            recv_sem=term_recv.at[k],
            device_id={"orb": peer},
            device_id_type=MESH,
        )

    def sum_copy(k):
        peer = (my_walk + k) % m
        return pltpu.make_async_remote_copy(
            src_ref=sums,
            dst_ref=sums_in.at[m - k],
            send_sem=sum_send.at[k],
            recv_sem=sum_recv.at[m - k],
            device_id={"walk": peer},
            device_id_type=MESH,
        )

    def sum_arrival(k):
        return pltpu.make_async_remote_copy(
            src_ref=sums,
            dst_ref=sums_in.at[k],
            send_sem=sum_send.at[k],
            recv_sem=sum_recv.at[k],
            device_id={"walk": (my_walk + k) % m},
            device_id_type=MESH,
        )

    add(0, 1)
    add_some(0, 0, steps - 1)
    for k in range(1, n):
        term_copy(k).start()
    for g in range(early, owned):
        send_vector(g)
    if owned > 1:
        finish(0)

    if owned > 2:
        def vector(g, _):
            add(g, 1)
            add_some(g, 0, steps - 1)
            finish(g)
            return _

        lax.fori_loop(1, owned - 1, vector, 0)

    def drain(g, _):
        def one(k, _):
            chunk_copy(g, k).wait_send()
            return _

        return lax.fori_loop(1, n, one, _)

    last = owned - 1
    lax.fori_loop(0, last, drain, 0)
    for k in range(1, m):
        walk_copy(k).wait_send()
    for k in range(1, n):
        term_copy(k).wait_send()

    mine = terms[me * share // LANES]
    for k in range(1, n):
        term_copy(k).wait_recv()
        mine = mine + terms_in[k]
    sums[...] = mine
    if owned > 1:
        add(last, 1)
    for k in range(1, m):
        sum_copy(k).start()
    if owned > 1:
        add_some(last, 0, steps - 2)
    total = sums[...]
    for k in range(1, m):
        sum_arrival(k).wait_recv()
        total = total + sums_in[k]
    offset = (me * share) % LANES + my_walk * (walkers * owned)
    total = pltpu.roll(jnp.broadcast_to(total, (8, LANES)), (LANES - offset) % LANES, 1)
    for w in range(walkers):
        bias_out[w : w + 1, :] = total[:1, w * owned : (w + 1) * owned] - shift[...]
    for k in range(1, m):
        sum_copy(k).wait_send()
    if owned > 1:
        add_some(last, steps - 2, steps - 1)
    finish(last)
    drain(last, 0)


def store(bias, rounded, bias_out, rotated, sems):
    owned = rounded.shape[0]
    writes = [
        pltpu.make_async_copy(rounded.at[g], rotated.at[g], sems.at[g]) for g in range(owned)
    ]
    writes.append(pltpu.make_async_copy(bias, bias_out, sems.at[owned]))
    for write in writes:
        write.start()
    for write in writes:
        write.wait()


def local(n, m, chol, orbitals, greens, shift):
    vectors, rows, cols = chol.shape
    owned = vectors // n
    walkers, occupied, _ = greens.shape
    bf16, f32 = jnp.bfloat16, jnp.float32
    dma = pltpu.SemaphoreType.DMA
    regular = pltpu.SemaphoreType.REGULAR
    any_space = pl.BlockSpec(memory_space=pl.ANY)
    vmem = pl.BlockSpec(memory_space=pltpu.VMEM)
    singles = n.bit_length() - 2
    packed = n * m * walkers * owned // LANES
    bias, rounded = pl.pallas_call(
        functools.partial(kernel, n, m),
        out_shape=(
            pltpu.VMEM((walkers, owned), f32),
            pltpu.VMEM((owned, occupied, cols), bf16),
        ),
        in_specs=[any_space] * 3 + [vmem],
        out_specs=(vmem, vmem),
        scratch_shapes=[
            pltpu.VMEM((n, owned, rows, cols), bf16),
            pltpu.VMEM((singles, rows, cols), bf16),
            pltpu.VMEM(chol.shape, bf16),
            pltpu.VMEM(orbitals.shape, bf16),
            pltpu.VMEM((n, occupied, rows), bf16),
            pltpu.VMEM(greens.shape, bf16),
            pltpu.VMEM((m, walkers, rows, cols), bf16),
            pltpu.VMEM((m, walkers, rows, cols), bf16),
            pltpu.VMEM((owned, occupied, cols), f32),
            pltpu.VMEM((packed * LANES, LANES), f32),
            pltpu.VMEM((packed, 1, LANES), f32),
            pltpu.VMEM((n, 1, LANES), f32),
            pltpu.VMEM((1, LANES), f32),
            pltpu.VMEM((m, 1, LANES), f32),
            dma((3 + singles,)),
            dma((n, owned)),
            dma((n, owned)),
            dma((m,)),
            dma((m,)),
            dma((n,)),
            dma((n,)),
            dma((m,)),
            dma((m,)),
            regular((n,)),
            regular((3,)),
        ],
        compiler_params=pltpu.CompilerParams(
            collective_id=0, has_side_effects=True, vmem_limit_bytes=59 * 2**20
        ),
    )(chol, orbitals, greens, shift.reshape(1, owned))
    return pl.pallas_call(
        store,
        out_shape=(
            jax.ShapeDtypeStruct((walkers, owned), f32),
            jax.ShapeDtypeStruct((owned, occupied, cols), bf16),
        ),
        in_specs=[vmem, vmem],
        out_specs=(any_space, any_space),
        scratch_shapes=[dma((owned + 1,))],
        compiler_params=pltpu.CompilerParams(vmem_limit_bytes=2**20),
    )(bias, rounded)


def solution(mesh):
    in_specs = (P(None, "orb", "walk"), P(), P("walk", None, None), P("orb"))
    out_specs = (P("walk", "orb"), P("orb", None, "walk"))
    body = functools.partial(local, mesh.shape["orb"], mesh.shape["walk"])
    return jax.shard_map(body, mesh=mesh, in_specs=in_specs, out_specs=out_specs, check_vma=False)
```

time: 104 us -> 99.6 us (0.958)
  Pallas kernels: 102 us -> 98.8 us
    pallas_call x1, Pallas kernels: 99.9 us -> 96.7 us  [local(): pl.pallas_call(functools.partial(kernel, n, m), out_shape=(pltpu.VMEM((wa...]
where the time goes in v1:
time: 99.6 us; the launch traced here: 99.4 us
  Pallas kernels  98.8 us (99%)
    pallas_call x1, Pallas kernels, local(): pl.pallas_call(functools.partial(kernel, n, m), out_shape=(pltpu.VMEM((wa...  96.7 us
    pallas_call x1, Pallas kernels, local(): pl.pallas_call(store, out_shape=(jax.ShapeDtypeStruct((walkers, owned), f...  2.05 us

profile of v1, /device:TPU:1, one launch (start us, length us, event | category | flops | bytes accessed | tf_op | source)
XLA Modules:
  0.0 99.4 jit_solution(12895471287801258430)
XLA Ops:
  0.6 96.7 %shard_map.59 = (f32[1,4]{1,0:T(1,128)S(1)}, bf16[4,1024,512]{2,1,0:T(8,128)(2,1)S(1)}) custom-call(bf16[32,256,512]{2,1,0:T(8,128)(2,1)} %chol.1, bf16[2048,1024]{1,0:T(8,128)(2,1)} %orbitals.1, bf16[1,1024,2048]{2,1,0:T(8,128)(2,1)} %greens.1, f32[1,4]{1,0:T(1,128)} %bitcast.1), custom_call_target="tpu_custom_call" | custom-call | tf_op jit(solution)/shard_map/pallas_call | solution.py:344
  97.4 2.1 %shard_map.60 = (f32[1,4]{1,0:T(1,128)}, bf16[4,1024,512]{2,1,0:T(8,128)(2,1)}) custom-call(f32[1,4]{1,0:T(1,128)S(1)} %get-tuple-element.4.bias, bf16[4,1024,512]{2,1,0:T(8,128)(2,1)S(1)} %get-tuple-element.5.rounded), custom_call_target="tpu_custom_call" | custom-call | tf_op jit(solution)/shard_map/pallas_call | solution.py:383

commit v2 on v1

--- a/solution.py
+++ b/solution.py
@@ -28,9 +28,10 @@
 
 
 def kernel(
-    n, m, chol, orbitals, greens, shift, bias_out, rotated,
+    n, m, chol, orbitals, greens, shift,
+    bias_out, rounded, acc_last, chunk_last, orb_last,
     chunks, first_v, chol_v, orb_v, orb_t, greens_v, products, arrived, acc,
-    rows_v, terms, terms_in, sums, sums_in,
+    rows_v, terms, terms_in, sums, sums_in, shift_v,
     local_sem, send_sem, recv_sem, walk_send, walk_recv,
     term_send, term_recv, sum_send, sum_recv, heard, chain,
 ):
@@ -55,7 +56,7 @@
     pl.when(leader & has_above)(lambda: greet(my_walk + 1))
 
     firsts = [
-        pltpu.make_async_copy(chol.at[xor(me, bit, n) * owned], first_v.at[i], local_sem.at[3 + i])
+        pltpu.make_async_copy(chol.at[xor(me, bit, n) * owned], first_v.at[i], local_sem.at[4 + i])
         for i, bit in enumerate(bits[1:])
     ]
     for load in firsts:
@@ -64,6 +65,7 @@
         pltpu.make_async_copy(greens, greens_v, local_sem.at[0]),
         pltpu.make_async_copy(orbitals, orb_v, local_sem.at[1]),
         pltpu.make_async_copy(chol, chol_v, local_sem.at[2]),
+        pltpu.make_async_copy(shift, shift_v, local_sem.at[3]),
     ]
 
     planes = (my_walk + m - 1) // m + (2 * m - 2 - my_walk) // m
@@ -83,11 +85,13 @@
     for bit in bits:
         hear(bit)
 
-    def chunk_copy(g, k, src=None):
+    last, final = owned - 1, 3
+
+    def chunk_copy(g, k, src=None, dst=None):
         peer = xor(me, k, n)
         return pltpu.make_async_remote_copy(
             src_ref=chol.at[peer * owned + g] if src is None else src,
-            dst_ref=chunks.at[k, g],
+            dst_ref=chunks.at[k, g] if dst is None else dst,
             send_sem=send_sem.at[k, g],
             recv_sem=recv_sem.at[k, g],
             device_id={"orb": peer},
@@ -99,7 +103,8 @@
             if low == 1:
                 chunk_copy(g, 1).start()
             for chip in range(half - 1, 0, -1):
-                chunk_copy(g, chip * 2 + low).start()
+                k = chip * 2 + low
+                chunk_copy(g, k, dst=chunk_last if (g, k) == (last, final) else None).start()
 
     for i, bit in enumerate(bits[1:]):
         firsts[i].wait()
@@ -147,6 +152,7 @@
         return _
 
     lax.fori_loop(0, n, turn, 0)
+    orb_last[...] = orb_t[xor(me, final, n)]
 
     def walk_copy(k):
         peer = (my_walk + k) % m
@@ -179,7 +185,10 @@
         acc[g] = jnp.dot(orb_t[me], chol_v[me * owned + g], preferred_element_type=jnp.float32)
         return _
 
-    lax.fori_loop(0, owned, begin, 0)
+    lax.fori_loop(0, last, begin, 0)
+    acc_last[...] = jnp.dot(
+        orb_t[me], chol_v[me * owned + last], preferred_element_type=jnp.float32
+    )
     arrived[0] = products[my_walk]
     for k in range(1, m):
         walk_arrival(k).wait_recv()
@@ -205,9 +214,7 @@
 
     def take(g, k):
         chunk_copy(g, k).wait_recv()
-        return acc[g] + jnp.dot(
-            orb_t[xor(me, k, n)], chunks[k, g], preferred_element_type=jnp.float32
-        )
+        return jnp.dot(orb_t[xor(me, k, n)], chunks[k, g], preferred_element_type=jnp.float32)
 
     def arrival(i):
         return (half - 1 - i % (half - 1)) * 2 + i // (half - 1)
@@ -215,7 +222,10 @@
     steps = 2 * (half - 1)
 
     def add(g, k):
-        acc[g] = take(g, k)
+        if isinstance(g, int) and g == last:
+            acc_last[...] += take(g, k)
+        else:
+            acc[g] += take(g, k)
 
     def add_some(g, start, stop):
         def step(i, _):
@@ -225,7 +235,7 @@
         lax.fori_loop(start, stop, step, 0)
 
     def finish(g):
-        rotated[g] = take(g, arrival(steps - 1)).astype(rotated.dtype)
+        rounded[g] = (acc[g] + take(g, arrival(steps - 1))).astype(rounded.dtype)
 
     def term_copy(k):
         peer = xor(me, k, n)
@@ -284,7 +294,6 @@
 
         return lax.fori_loop(1, n, one, _)
 
-    last = owned - 1
     lax.fori_loop(0, last, drain, 0)
     for k in range(1, m):
         walk_copy(k).wait_send()
@@ -302,6 +311,7 @@
         sum_copy(k).start()
     if owned > 1:
         add_some(last, 0, steps - 2)
+    loads[3].wait()
     total = sums[...]
     for k in range(1, m):
         sum_arrival(k).wait_recv()
@@ -309,22 +319,27 @@
     offset = (me * share) % LANES + my_walk * (walkers * owned)
     total = pltpu.roll(jnp.broadcast_to(total, (8, LANES)), (LANES - offset) % LANES, 1)
     for w in range(walkers):
-        bias_out[w : w + 1, :] = total[:1, w * owned : (w + 1) * owned] - shift[...]
+        bias_out[w : w + 1, :] = total[:1, w * owned : (w + 1) * owned] - shift_v[...]
     for k in range(1, m):
         sum_copy(k).wait_send()
     if owned > 1:
         add_some(last, steps - 2, steps - 1)
-    finish(last)
+    chunk_copy(last, final, dst=chunk_last).wait_recv()
     drain(last, 0)
 
 
-def store(bias, rounded, bias_out, rotated, sems):
-    owned = rounded.shape[0]
-    writes = [
-        pltpu.make_async_copy(rounded.at[g], rotated.at[g], sems.at[g]) for g in range(owned)
-    ]
-    writes.append(pltpu.make_async_copy(bias, bias_out, sems.at[owned]))
-    for write in writes:
+def store(bias, rounded, acc_last, chunk_last, orb_last, bias_out, rotated, last_v, sems):
+    last = rounded.shape[0]
+    writes = [pltpu.make_async_copy(rounded.at[g], rotated.at[g], sems.at[g]) for g in range(last)]
+    writes.append(pltpu.make_async_copy(last_v, rotated.at[last], sems.at[last]))
+    writes.append(pltpu.make_async_copy(bias, bias_out, sems.at[last + 1]))
+    for write in writes[:last]:
+        write.start()
+    last_v[...] = (
+        acc_last[...]
+        + jnp.dot(orb_last[...], chunk_last[...], preferred_element_type=jnp.float32)
+    ).astype(last_v.dtype)
+    for write in writes[last:]:
         write.start()
     for write in writes:
         write.wait()
@@ -341,14 +356,17 @@
     vmem = pl.BlockSpec(memory_space=pltpu.VMEM)
     singles = n.bit_length() - 2
     packed = n * m * walkers * owned // LANES
-    bias, rounded = pl.pallas_call(
+    carried = pl.pallas_call(
         functools.partial(kernel, n, m),
         out_shape=(
             pltpu.VMEM((walkers, owned), f32),
-            pltpu.VMEM((owned, occupied, cols), bf16),
+            pltpu.VMEM((owned - 1, occupied, cols), bf16),
+            pltpu.VMEM((occupied, cols), f32),
+            pltpu.VMEM((rows, cols), bf16),
+            pltpu.VMEM((occupied, rows), bf16),
         ),
-        in_specs=[any_space] * 3 + [vmem],
-        out_specs=(vmem, vmem),
+        in_specs=[any_space] * 4,
+        out_specs=(vmem,) * 5,
         scratch_shapes=[
             pltpu.VMEM((n, owned, rows, cols), bf16),
             pltpu.VMEM((singles, rows, cols), bf16),
@@ -358,13 +376,14 @@
             pltpu.VMEM(greens.shape, bf16),
             pltpu.VMEM((m, walkers, rows, cols), bf16),
             pltpu.VMEM((m, walkers, rows, cols), bf16),
-            pltpu.VMEM((owned, occupied, cols), f32),
+            pltpu.VMEM((owned - 1, occupied, cols), f32),
             pltpu.VMEM((packed * LANES, LANES), f32),
             pltpu.VMEM((packed, 1, LANES), f32),
             pltpu.VMEM((n, 1, LANES), f32),
             pltpu.VMEM((1, LANES), f32),
             pltpu.VMEM((m, 1, LANES), f32),
-            dma((3 + singles,)),
+            pltpu.VMEM((1, owned), f32),
+            dma((4 + singles,)),
             dma((n, owned)),
             dma((n, owned)),
             dma((m,)),
@@ -377,7 +396,7 @@
             regular((3,)),
         ],
         compiler_params=pltpu.CompilerParams(
-            collective_id=0, has_side_effects=True, vmem_limit_bytes=59 * 2**20
+            collective_id=0, has_side_effects=True, vmem_limit_bytes=56 * 2**20
         ),
     )(chol, orbitals, greens, shift.reshape(1, owned))
     return pl.pallas_call(
@@ -386,11 +405,11 @@
             jax.ShapeDtypeStruct((walkers, owned), f32),
             jax.ShapeDtypeStruct((owned, occupied, cols), bf16),
         ),
-        in_specs=[vmem, vmem],
+        in_specs=[vmem] * 5,
         out_specs=(any_space, any_space),
-        scratch_shapes=[dma((owned + 1,))],
-        compiler_params=pltpu.CompilerParams(vmem_limit_bytes=2**20),
-    )(bias, rounded)
+        scratch_shapes=[pltpu.VMEM((occupied, cols), bf16), dma((owned + 1,))],
+        compiler_params=pltpu.CompilerParams(vmem_limit_bytes=8 * 2**20),
+    )(*carried)
 
 
 def solution(mesh):

time: 99.6 us -> 98.6 us (0.990)
  Pallas kernels: 98.8 us -> 97.8 us
    pallas_call x1, Pallas kernels: 96.7 us -> 95.7 us  [local(): pl.pallas_call(functools.partial(kernel, n, m), out_shape=(pltpu.VMEM((wa...]
where the time goes in v2:
time: 98.6 us; the launch traced here: 98.4 us
  Pallas kernels  97.8 us (99%)
    pallas_call x1, Pallas kernels, local(): pl.pallas_call(functools.partial(kernel, n, m), out_shape=(pltpu.VMEM((wa...  95.7 us
    pallas_call x1, Pallas kernels, local(): pl.pallas_call(store, out_shape=(jax.ShapeDtypeStruct((walkers, owned), f...  2.07 us

profile of v2, /device:TPU:1, one launch (start us, length us, event | category | flops | bytes accessed | tf_op | source)
XLA Modules:
  0.0 98.4 jit_solution(12401408724866764000)
XLA Ops:
  0.6 95.7 %shard_map.59 = (f32[1,4]{1,0:T(1,128)S(1)}, bf16[3,1024,512]{2,1,0:T(8,128)(2,1)S(1)}, f32[1024,512]{1,0:T(8,128)S(1)}, bf16[256,512]{1,0:T(8,128)(2,1)S(1)}, bf16[1024,256]{1,0:T(8,128)(2,1)S(1)}) custom-call(bf16[32,256,512]{2,1,0:T(8,128)(2,1)} %chol.1, bf16[2048,1024]{1,0:T(8,128)(2,1)} %orbitals.1, bf16[1,1024,2048]{2,1,0:T(8,128)(2,1)} %greens.1, ...), custom_call_target="tpu_custom_call" | custom-call | tf_op jit(solution)/shard_map/pallas_call | solution.py:359
  96.3 2.1 %shard_map.60 = (f32[1,4]{1,0:T(1,128)}, bf16[4,1024,512]{2,1,0:T(8,128)(2,1)}) custom-call(f32[1,4]{1,0:T(1,128)S(1)} %get-tuple-element.7.bias, bf16[3,1024,512]{2,1,0:T(8,128)(2,1)S(1)} %get-tuple-element.8.rounded, f32[1024,512]{1,0:T(8,128)S(1)} %get-tuple-element.9.acc_last, bf16[256,512]{1,0:T(8,128)(2,1)S(1)} %get-tuple-element.10.chunk_last, ...), custom_call_target="tpu_custom_call" | custom-call | tf_op jit(solution)/shard_map/pallas_call | solution.py:402

commit v3 on v2

--- a/solution.py
+++ b/solution.py
@@ -40,14 +40,24 @@
     owned = vectors // n
     walkers = greens.shape[0]
     half = n // 2
+    core = me % 2
+    last, final = owned - 1, 3
     leader = me == n - 1
     has_below, has_above = my_walk > 0, my_walk < m - 1
     bits = [1 << b for b in range(n.bit_length() - 1)]
     share = m * walkers * owned
 
+    def is_set(bit):
+        return (me // bit) % 2
+
     barrier = pltpu.get_barrier_semaphore()
-    for bit in reversed(bits):
+
+    def greet_orb(bit):
         pl.semaphore_signal(barrier, inc=1, device_id={"orb": xor(me, bit, n)}, device_id_type=MESH)
+
+    for bit in reversed(bits[1:]):
+        pl.when(is_set(bit) == 0)(functools.partial(greet_orb, bit))
+    greet_orb(1)
 
     def greet(other):
         pl.semaphore_signal(barrier, inc=1, device_id={"walk": other}, device_id_type=MESH)
@@ -62,35 +72,20 @@
     for load in firsts:
         load.start()
     loads = [
-        pltpu.make_async_copy(greens, greens_v, local_sem.at[0]),
+        pltpu.make_async_copy(chol, chol_v, local_sem.at[0]),
         pltpu.make_async_copy(orbitals, orb_v, local_sem.at[1]),
-        pltpu.make_async_copy(chol, chol_v, local_sem.at[2]),
+        pltpu.make_async_copy(greens, greens_v, local_sem.at[2]),
         pltpu.make_async_copy(shift, shift_v, local_sem.at[3]),
     ]
 
     planes = (my_walk + m - 1) // m + (2 * m - 2 - my_walk) // m
-    pl.semaphore_wait(barrier, len(bits) + me // (n - 1) * planes)
-
-    def tell(k):
-        peer = xor(me, low_bit(k), n)
-        pl.semaphore_signal(heard.at[k], inc=1, device_id={"orb": peer}, device_id_type=MESH)
-
-    def hear(k):
-        if ones(k) > 1:
-            pl.semaphore_wait(heard.at[k], 1)
-        for further in range(k + 1, n):
-            if ones(further) == ones(k) + 1 and further - low_bit(further) == k:
-                tell(further)
-
-    for bit in bits:
-        hear(bit)
-
-    last, final = owned - 1, 3
+    pl.semaphore_wait(barrier, 1 + sum(is_set(bit) for bit in bits[1:]) + me // (n - 1) * planes)
 
     def chunk_copy(g, k, src=None, dst=None):
         peer = xor(me, k, n)
-        return pltpu.make_async_remote_copy(
-            src_ref=chol.at[peer * owned + g] if src is None else src,
+        source = chol if isinstance(g, int) and g == 0 else chol_v
+        return pltpu.make_async_remote_copy(
+            src_ref=source.at[peer * owned + g] if src is None else src,
             dst_ref=chunks.at[k, g] if dst is None else dst,
             send_sem=send_sem.at[k, g],
             recv_sem=recv_sem.at[k, g],
@@ -102,25 +97,49 @@
         for low in range(2):
             if low == 1:
                 chunk_copy(g, 1).start()
-            for chip in range(half - 1, 0, -1):
-                k = chip * 2 + low
-                chunk_copy(g, k, dst=chunk_last if (g, k) == (last, final) else None).start()
-
-    for i, bit in enumerate(bits[1:]):
+            for high in range(1, half):
+                if g == last and low == 1:
+                    k = (half - high) * 2 + low
+                    chunk_copy(g, k, dst=chunk_last if k == final else None).start()
+                else:
+                    chunk_copy(g, (high + core * (half - 2 * high)) * 2 + low).start()
+
+    def tell(k):
+        peer = xor(me, low_bit(k), n)
+        pl.semaphore_signal(heard.at[k], inc=1, device_id={"orb": peer}, device_id_type=MESH)
+
+    def hear(k):
+        pl.semaphore_wait(heard.at[k], 1)
+
+    def pass_along(k):
+        for further in range(k + 1, n):
+            if ones(further) == ones(k) + 1 and further - low_bit(further) == k:
+                tell(further)
+
+    def send_first(i, bit):
         firsts[i].wait()
         chunk_copy(0, bit, first_v.at[i]).start()
+
+    for bit in reversed(bits[1:]):
+        pl.when(is_set(bit) == 1)(functools.partial(tell, bit))
+    for i, bit in enumerate(bits[1:]):
+        pl.when(is_set(bit) == 1)(functools.partial(send_first, i, bit))
+    for i, bit in enumerate(bits[1:]):
+        pl.when(is_set(bit) == 0)(functools.partial(hear, bit))
+        pl.when(is_set(bit) == 0)(functools.partial(send_first, i, bit))
+        pass_along(bit)
     chunk_copy(0, 1).start()
     for low in range(2):
         for k in range(2 + low, n, 2):
             if ones(k) > 1:
                 hear(k)
+                pass_along(k)
                 chunk_copy(0, k).start()
-    early = max(owned - 1, 1)
-    for g in range(1, early):
-        send_vector(g)
-
     for load in loads:
         load.start()
+    loads[0].wait()
+    for g in range(1, last):
+        send_vector(g)
 
     def pass_on(i, other):
         pl.semaphore_signal(chain.at[i], inc=1, device_id={"walk": other}, device_id_type=MESH)
@@ -137,8 +156,8 @@
                 chain.at[2], inc=1, device_id={"orb": xor(me, k, n)}, device_id_type=MESH
             )
 
-    loads[0].wait()
     loads[1].wait()
+    loads[2].wait()
     my_rows = orb_v[pl.ds(pl.multiple_of(me * rows, rows), rows), :]
     for w in range(walkers):
         for j in range(m):
@@ -178,8 +197,6 @@
     pl.when(me < n - 1)(lambda: pl.semaphore_wait(chain.at[2], 1))
     for k in range(1, m):
         walk_copy(k).start()
-
-    loads[2].wait()
 
     def begin(g, _):
         acc[g] = jnp.dot(orb_t[me], chol_v[me * owned + g], preferred_element_type=jnp.float32)
@@ -273,10 +290,8 @@
     add_some(0, 0, steps - 1)
     for k in range(1, n):
         term_copy(k).start()
-    for g in range(early, owned):
-        send_vector(g)
-    if owned > 1:
-        finish(0)
+    send_vector(last)
+    finish(0)
 
     if owned > 2:
         def vector(g, _):
@@ -305,12 +320,10 @@
         term_copy(k).wait_recv()
         mine = mine + terms_in[k]
     sums[...] = mine
-    if owned > 1:
-        add(last, 1)
+    add(last, 1)
     for k in range(1, m):
         sum_copy(k).start()
-    if owned > 1:
-        add_some(last, 0, steps - 2)
+    add_some(last, 0, steps - 2)
     loads[3].wait()
     total = sums[...]
     for k in range(1, m):
@@ -322,10 +335,16 @@
         bias_out[w : w + 1, :] = total[:1, w * owned : (w + 1) * owned] - shift_v[...]
     for k in range(1, m):
         sum_copy(k).wait_send()
-    if owned > 1:
-        add_some(last, steps - 2, steps - 1)
+    add_some(last, steps - 2, steps - 1)
+
+    def settle(i, _):
+        chunk_copy(last, arrival(i)).wait_send()
+        return _
+
+    chunk_copy(last, 1).wait_send()
+    lax.fori_loop(0, steps - 2, settle, 0)
     chunk_copy(last, final, dst=chunk_last).wait_recv()
-    drain(last, 0)
+    lax.fori_loop(steps - 2, steps, settle, 0)
 
 
 def store(bias, rounded, acc_last, chunk_last, orb_last, bias_out, rotated, last_v, sems):

time: 98.6 us -> 98.5 us (level)
  no operation moved by 1% of the time
where the time goes in v3:
time: 98.5 us; the launch traced here: 98.3 us
  Pallas kernels  97.7 us (99%)
    pallas_call x1, Pallas kernels, local(): pl.pallas_call(functools.partial(kernel, n, m), out_shape=(pltpu.VMEM((wa...  95.6 us
    pallas_call x1, Pallas kernels, local(): pl.pallas_call(store, out_shape=(jax.ShapeDtypeStruct((walkers, owned), f...  2.07 us

profile of v3, /device:TPU:1, one launch (start us, length us, event | category | flops | bytes accessed | tf_op | source)
XLA Modules:
  0.0 98.3 jit_solution(9426832792219643837)
XLA Ops:
  0.6 95.6 %shard_map.59 = (f32[1,4]{1,0:T(1,128)S(1)}, bf16[3,1024,512]{2,1,0:T(8,128)(2,1)S(1)}, f32[1024,512]{1,0:T(8,128)S(1)}, bf16[256,512]{1,0:T(8,128)(2,1)S(1)}, bf16[1024,256]{1,0:T(8,128)(2,1)S(1)}) custom-call(bf16[32,256,512]{2,1,0:T(8,128)(2,1)} %chol.1, bf16[2048,1024]{1,0:T(8,128)(2,1)} %orbitals.1, bf16[1,1024,2048]{2,1,0:T(8,128)(2,1)} %greens.1, ...), custom_call_target="tpu_custom_call" | custom-call | tf_op jit(solution)/shard_map/pallas_call | solution.py:378
  96.2 2.1 %shard_map.60 = (f32[1,4]{1,0:T(1,128)}, bf16[4,1024,512]{2,1,0:T(8,128)(2,1)}) custom-call(f32[1,4]{1,0:T(1,128)S(1)} %get-tuple-element.7.bias, bf16[3,1024,512]{2,1,0:T(8,128)(2,1)S(1)} %get-tuple-element.8.rounded, f32[1024,512]{1,0:T(8,128)S(1)} %get-tuple-element.9.acc_last, bf16[256,512]{1,0:T(8,128)(2,1)S(1)} %get-tuple-element.10.chunk_last, ...), custom_call_target="tpu_custom_call" | custom-call | tf_op jit(solution)/shard_map/pallas_call | solution.py:421

commit v4 on v3

--- a/solution.py
+++ b/solution.py
@@ -41,7 +41,7 @@
     walkers = greens.shape[0]
     half = n // 2
     core = me % 2
-    last, final = owned - 1, 3
+    last, finals = owned - 1, (5, 3)
     leader = me == n - 1
     has_below, has_above = my_walk > 0, my_walk < m - 1
     bits = [1 << b for b in range(n.bit_length() - 1)]
@@ -93,6 +93,9 @@
             device_id_type=MESH,
         )
 
+    def place(k):
+        return chunk_last.at[pl.ds(finals.index(k) * rows, rows)]
+
     def send_vector(g):
         for low in range(2):
             if low == 1:
@@ -100,7 +103,7 @@
             for high in range(1, half):
                 if g == last and low == 1:
                     k = (half - high) * 2 + low
-                    chunk_copy(g, k, dst=chunk_last if k == final else None).start()
+                    chunk_copy(g, k, dst=place(k) if k in finals else None).start()
                 else:
                     chunk_copy(g, (high + core * (half - 2 * high)) * 2 + low).start()
 
@@ -171,7 +174,8 @@
         return _
 
     lax.fori_loop(0, n, turn, 0)
-    orb_last[...] = orb_t[xor(me, final, n)]
+    for i, k in enumerate(finals):
+        orb_last[:, i * rows : (i + 1) * rows] = orb_t[xor(me, k, n)]
 
     def walk_copy(k):
         peer = (my_walk + k) % m
@@ -335,7 +339,6 @@
         bias_out[w : w + 1, :] = total[:1, w * owned : (w + 1) * owned] - shift_v[...]
     for k in range(1, m):
         sum_copy(k).wait_send()
-    add_some(last, steps - 2, steps - 1)
 
     def settle(i, _):
         chunk_copy(last, arrival(i)).wait_send()
@@ -343,23 +346,28 @@
 
     chunk_copy(last, 1).wait_send()
     lax.fori_loop(0, steps - 2, settle, 0)
-    chunk_copy(last, final, dst=chunk_last).wait_recv()
+    for k in finals:
+        chunk_copy(last, k, dst=place(k)).wait_recv()
     lax.fori_loop(steps - 2, steps, settle, 0)
 
 
 def store(bias, rounded, acc_last, chunk_last, orb_last, bias_out, rotated, last_v, sems):
     last = rounded.shape[0]
+    height = last_v.shape[0] // 2
     writes = [pltpu.make_async_copy(rounded.at[g], rotated.at[g], sems.at[g]) for g in range(last)]
-    writes.append(pltpu.make_async_copy(last_v, rotated.at[last], sems.at[last]))
-    writes.append(pltpu.make_async_copy(bias, bias_out, sems.at[last + 1]))
-    for write in writes[:last]:
+    writes.append(pltpu.make_async_copy(bias, bias_out, sems.at[last]))
+    for write in writes:
         write.start()
-    last_v[...] = (
-        acc_last[...]
-        + jnp.dot(orb_last[...], chunk_last[...], preferred_element_type=jnp.float32)
-    ).astype(last_v.dtype)
-    for write in writes[last:]:
-        write.start()
+    for i in range(2):
+        span = pl.ds(i * height, height)
+        last_v[span, :] = (
+            acc_last[span, :]
+            + jnp.dot(orb_last[span, :], chunk_last[...], preferred_element_type=jnp.float32)
+        ).astype(last_v.dtype)
+        writes.append(
+            pltpu.make_async_copy(last_v.at[span], rotated.at[last, span], sems.at[last + 1 + i])
+        )
+        writes[-1].start()
     for write in writes:
         write.wait()
 
@@ -381,8 +389,8 @@
             pltpu.VMEM((walkers, owned), f32),
             pltpu.VMEM((owned - 1, occupied, cols), bf16),
             pltpu.VMEM((occupied, cols), f32),
-            pltpu.VMEM((rows, cols), bf16),
-            pltpu.VMEM((occupied, rows), bf16),
+            pltpu.VMEM((2 * rows, cols), bf16),
+            pltpu.VMEM((occupied, 2 * rows), bf16),
         ),
         in_specs=[any_space] * 4,
         out_specs=(vmem,) * 5,
@@ -426,7 +434,7 @@
         ),
         in_specs=[vmem] * 5,
         out_specs=(any_space, any_space),
-        scratch_shapes=[pltpu.VMEM((occupied, cols), bf16), dma((owned + 1,))],
+        scratch_shapes=[pltpu.VMEM((occupied, cols), bf16), dma((owned + 2,))],
         compiler_params=pltpu.CompilerParams(vmem_limit_bytes=8 * 2**20),
     )(*carried)
 

time: 98.5 us -> 98.1 us (level)
  no operation moved by 1% of the time
where the time goes in v4:
time: 98.1 us; the launch traced here: 98 us
  Pallas kernels  97.4 us (99%)
    pallas_call x1, Pallas kernels, local(): pl.pallas_call(functools.partial(kernel, n, m), out_shape=(pltpu.VMEM((wa...  95.3 us
    pallas_call x1, Pallas kernels, local(): pl.pallas_call(store, out_shape=(jax.ShapeDtypeStruct((walkers, owned), f...  2.08 us

profile of v4, /device:TPU:1, one launch (start us, length us, event | category | flops | bytes accessed | tf_op | source)
XLA Modules:
  0.0 98.0 jit_solution(16177680606011427145)
XLA Ops:
  0.6 95.3 %shard_map.59 = (f32[1,4]{1,0:T(1,128)S(1)}, bf16[3,1024,512]{2,1,0:T(8,128)(2,1)S(1)}, f32[1024,512]{1,0:T(8,128)S(1)}, bf16[512,512]{1,0:T(8,128)(2,1)S(1)}, bf16[1024,512]{1,0:T(8,128)(2,1)S(1)}) custom-call(bf16[32,256,512]{2,1,0:T(8,128)(2,1)} %chol.1, bf16[2048,1024]{1,0:T(8,128)(2,1)} %orbitals.1, bf16[1,1024,2048]{2,1,0:T(8,128)(2,1)} %greens.1, ...), custom_call_target="tpu_custom_call" | custom-call | tf_op jit(solution)/shard_map/pallas_call | solution.py:386
  95.9 2.1 %shard_map.60 = (f32[1,4]{1,0:T(1,128)}, bf16[4,1024,512]{2,1,0:T(8,128)(2,1)}) custom-call(f32[1,4]{1,0:T(1,128)S(1)} %get-tuple-element.7.bias, bf16[3,1024,512]{2,1,0:T(8,128)(2,1)S(1)} %get-tuple-element.8.rounded, f32[1024,512]{1,0:T(8,128)S(1)} %get-tuple-element.9.acc_last, bf16[512,512]{1,0:T(8,128)(2,1)S(1)} %get-tuple-element.10.chunk_last, ...), custom_call_target="tpu_custom_call" | custom-call | tf_op jit(solution)/shard_map/pallas_call | solution.py:429

commit v5 on v4

--- a/solution.py
+++ b/solution.py
@@ -50,27 +50,28 @@
     def is_set(bit):
         return (me // bit) % 2
 
-    barrier = pltpu.get_barrier_semaphore()
-
-    def greet_orb(bit):
-        pl.semaphore_signal(barrier, inc=1, device_id={"orb": xor(me, bit, n)}, device_id_type=MESH)
-
-    for bit in reversed(bits[1:]):
-        pl.when(is_set(bit) == 0)(functools.partial(greet_orb, bit))
-    greet_orb(1)
-
-    def greet(other):
-        pl.semaphore_signal(barrier, inc=1, device_id={"walk": other}, device_id_type=MESH)
-
-    pl.when(leader & has_below)(lambda: greet(my_walk - 1))
-    pl.when(leader & has_above)(lambda: greet(my_walk + 1))
-
     firsts = [
         pltpu.make_async_copy(chol.at[xor(me, bit, n) * owned], first_v.at[i], local_sem.at[4 + i])
         for i, bit in enumerate(bits[1:])
     ]
     for load in firsts:
         load.start()
+
+    barrier = pltpu.get_barrier_semaphore()
+
+    def greet_orb(bit):
+        pl.semaphore_signal(barrier, inc=1, device_id={"orb": xor(me, bit, n)}, device_id_type=MESH)
+
+    for bit in reversed(bits[1:]):
+        pl.when(is_set(bit) == 0)(functools.partial(greet_orb, bit))
+    greet_orb(1)
+
+    def greet(other):
+        pl.semaphore_signal(barrier, inc=1, device_id={"walk": other}, device_id_type=MESH)
+
+    pl.when(leader & has_below)(lambda: greet(my_walk - 1))
+    pl.when(leader & has_above)(lambda: greet(my_walk + 1))
+
     loads = [
         pltpu.make_async_copy(chol, chol_v, local_sem.at[0]),
         pltpu.make_async_copy(orbitals, orb_v, local_sem.at[1]),

time: 98.1 us -> 98.1 us (level)
  no operation moved by 1% of the time
where the time goes in v5:
time: 98.1 us; the launch traced here: 97.9 us
  Pallas kernels  97.3 us (99%)
    pallas_call x1, Pallas kernels, local(): pl.pallas_call(functools.partial(kernel, n, m), out_shape=(pltpu.VMEM((wa...  95.2 us
    pallas_call x1, Pallas kernels, local(): pl.pallas_call(store, out_shape=(jax.ShapeDtypeStruct((walkers, owned), f...  2.08 us

profile of v5, /device:TPU:1, one launch (start us, length us, event | category | flops | bytes accessed | tf_op | source)
XLA Modules:
  0.0 97.9 jit_solution(3981819770137579747)
XLA Ops:
  0.6 95.2 %shard_map.59 = (f32[1,4]{1,0:T(1,128)S(1)}, bf16[3,1024,512]{2,1,0:T(8,128)(2,1)S(1)}, f32[1024,512]{1,0:T(8,128)S(1)}, bf16[512,512]{1,0:T(8,128)(2,1)S(1)}, bf16[1024,512]{1,0:T(8,128)(2,1)S(1)}) custom-call(bf16[32,256,512]{2,1,0:T(8,128)(2,1)} %chol.1, bf16[2048,1024]{1,0:T(8,128)(2,1)} %orbitals.1, bf16[1,1024,2048]{2,1,0:T(8,128)(2,1)} %greens.1, ...), custom_call_target="tpu_custom_call" | custom-call | tf_op jit(solution)/shard_map/pallas_call | solution.py:387
  95.9 2.1 %shard_map.60 = (f32[1,4]{1,0:T(1,128)}, bf16[4,1024,512]{2,1,0:T(8,128)(2,1)}) custom-call(f32[1,4]{1,0:T(1,128)S(1)} %get-tuple-element.7.bias, bf16[3,1024,512]{2,1,0:T(8,128)(2,1)S(1)} %get-tuple-element.8.rounded, f32[1024,512]{1,0:T(8,128)S(1)} %get-tuple-element.9.acc_last, bf16[512,512]{1,0:T(8,128)(2,1)S(1)} %get-tuple-element.10.chunk_last, ...), custom_call_target="tpu_custom_call" | custom-call | tf_op jit(solution)/shard_map/pallas_call | solution.py:430
